TPU v7x, 32 devices: a whole 2x2x4 slice. The times are simulated.
32 devices in a mesh: groups: 2 (over y), rows: 4 (over z), cols: 2 (over x), sub: 2 (over core).
Axes of the slice: x: 2, y: 2, z: 4, core: 2. Of those that a mesh axis runs over, the one named last changes fastest.
Arguments:
- stored_vectors: bfloat16 [3072, 8192], P(('cols', 'sub'), ('groups', 'rows')), parts along dimension 1, may hold values from -0.59765625 to 0.59765625
- previous_columns: bfloat16 [8192, 256], P(('groups', 'rows', 'cols', 'sub')), parts along dimension 0, may hold values from -3 to 3
- pivots: int32 [512], P('groups'), parts along dimension 0, may hold values from 0 to 4095, as said below
- diagonal: float32 [8192], P(('groups', 'rows', 'cols', 'sub')), parts along dimension 0, may hold values from 2 to 32
- ket_blocks: bfloat16 [128, 128, 256], P(('groups', 'rows', 'cols', 'sub')), parts along dimension 0, may hold values from -6 to 6
- shell_tags: int32 [128, 128], P(('groups', 'rows', 'cols', 'sub')), parts along dimension 0, may hold values from 0 to 3
- target_blocks: int32 [32, 4], P('groups'), parts along dimension 0, may hold values from 0 to 31, as said below
- block_counts: int32 [32], P('groups'), parts along dimension 0, may hold values from 0 to 4, as said below
- shell_norms: float32 [4], replicated, may hold values from 0.5 to 2
Outputs:
- new_vectors: bfloat16 [8192, 256], P(('groups', 'rows', 'cols', 'sub')), parts along dimension 0
- diag_out: float32 [8192], P(('groups', 'rows', 'cols', 'sub')), parts along dimension 0
- next_columns: bfloat16 [8192, 256], P(('groups', 'rows', 'cols', 'sub')), parts along dimension 0
There are 2 independent parts, one for each index of `groups`. A program takes and returns all parts, laid end to end along the dimension named above; an argument that names none is the same for every part. Nothing has to cross between parts.
Inputs may be any that keep to these rules, and one draw needn't show every extreme that they name: `pivots`: 256 distinct AO pairs. `target_blocks`: the used slots of all owners name every block of the 32 blocks exactly once; a used slot's block lies on a device with the owner's cols and sub indices (blocks g * 2 to g * 2 + 1 lie on the device of linear index g, rows slowest; owner o is the device of linear index o). At most 1 of one owner's used slots go to one device, and some owner reaches that in every draw. Entries of unused slots are arbitrary blocks. `block_counts`: some owner uses all 4 slots in every draw.
All inputs are finite; a program needn't handle non-finite values.
Results may differ from a plain program's by a relative error of at most 0.0004.
Values may be sent and summed in bfloat16 or wider, within the bound.
A program may use at most 64 MiB of HBM per device.

v0:
```python
import jax
import jax.numpy as jnp
from jax import lax
from jax.sharding import PartitionSpec as P


def slot_plan(row_targets, count, column_size, per_device):
    slot_count = row_targets.shape[0]
    slots = jnp.arange(slot_count, dtype=jnp.int32)
    valid = slots < count
    receiver = row_targets // (column_size * per_device)
    within = row_targets % per_device
    earlier = (
        (receiver[:, None] == receiver[None, :])
        & valid[:, None]
        & valid[None, :]
        & (slots[None, :] < slots[:, None])
    )
    ranking = jnp.sum(earlier.astype(jnp.int32), axis=1)
    return (valid, receiver, ranking, within)


def body(
    stored_vectors,
    previous_columns,
    pivots,
    diagonal,
    ket_blocks,
    shell_tags,
    target_blocks,
    block_counts,
    shell_norms,
):
    rows_here = previous_columns.shape[0]
    batch = previous_columns.shape[1]
    block_rows = ket_blocks.shape[1]
    slot_count = ket_blocks.shape[0]
    per_device = rows_here // block_rows
    band_rows = stored_vectors.shape[1]
    band_index = lax.axis_index("rows")
    device_index = lax.axis_index(("rows", "cols", "sub"))
    column_index = lax.axis_index(("cols", "sub"))
    column_size = lax.axis_size(("cols", "sub"))
    band_size = lax.axis_size("rows")
    peer_slots = (slot_count + band_size - 1) // band_size
    local_pivots = pivots - device_index * rows_here
    matches = jnp.arange(rows_here, dtype=jnp.int32)[:, None] == local_pivots[None, :]
    diag_terms = jnp.sum(jnp.where(matches, diagonal[:, None], jnp.float32(0.0)), axis=0)
    pivot_diag = lax.psum(diag_terms, ("rows", "cols", "sub"))
    band_pivots = pivots - band_index * band_rows
    inside = (band_pivots >= 0) & (band_pivots < band_rows)
    clamped = jnp.clip(band_pivots, 0, band_rows - 1)
    taken = jnp.take(stored_vectors, clamped, axis=1).astype(jnp.float32)
    picked = jnp.where(inside[None, :], taken, jnp.float32(0.0))
    pivot_rows = lax.psum(picked, "rows").astype(jnp.bfloat16)
    kinds = jnp.arange(shell_norms.shape[0], dtype=jnp.int32)
    factor = jnp.sum(
        jnp.where(shell_tags[..., None] == kinds, shell_norms, jnp.float32(0.0)), axis=-1
    )
    fresh = (ket_blocks.astype(jnp.float32) * factor[..., None]).astype(jnp.bfloat16)
    own_targets = lax.dynamic_index_in_dim(target_blocks, device_index, 0, keepdims=False)
    own_count = lax.dynamic_index_in_dim(block_counts, device_index, 0, keepdims=False)
    valid, receiver, ranking, within = slot_plan(own_targets, own_count, column_size, per_device)
    lines = jnp.arange(band_size * peer_slots, dtype=jnp.int32)[:, None]
    routing = (
        (lines // peer_slots == receiver[None, :])
        & (lines % peer_slots == ranking[None, :])
        & valid[None, :]
    ).astype(jnp.bfloat16)
    outgoing = jnp.dot(
        routing, fresh.reshape(slot_count, block_rows * batch), preferred_element_type=jnp.float32
    )
    outgoing = outgoing.astype(jnp.bfloat16).reshape(band_size, peer_slots, block_rows, batch)
    incoming = lax.all_to_all(outgoing, "rows", split_axis=0, concat_axis=0, tiled=True)
    sources = jnp.arange(band_size, dtype=jnp.int32) * column_size + column_index
    source_targets = jnp.take(target_blocks, sources, axis=0)
    source_counts = jnp.take(block_counts, sources, axis=0)
    plan_each = jax.vmap(
        lambda row_targets, count: slot_plan(row_targets, count, column_size, per_device)
    )
    source_valid, source_receiver, source_rank, source_within = plan_each(
        source_targets, source_counts
    )
    arriving = source_valid & (source_receiver == band_index)
    places = jnp.arange(per_device, dtype=jnp.int32)[:, None, None, None]
    peer_lines = jnp.arange(peer_slots, dtype=jnp.int32)[None, None, :, None]
    hits = (
        (source_within[None, :, None, :] == places)
        & (source_rank[None, :, None, :] == peer_lines)
        & arriving[None, :, None, :]
    )
    placement = (
        jnp.any(hits, axis=3).astype(jnp.bfloat16).reshape(per_device, band_size * peer_slots)
    )
    arranged = jnp.dot(
        placement,
        incoming.reshape(band_size * peer_slots, block_rows * batch),
        preferred_element_type=jnp.float32,
    )
    next_columns = arranged.astype(jnp.bfloat16).reshape(rows_here, batch)
    product = lax.psum_scatter(
        lax.dot_general(
            stored_vectors, pivot_rows, (((0,), (0,)), ((), ())), preferred_element_type=jnp.float32
        ),
        ("cols", "sub"),
        scatter_dimension=0,
        tiled=True,
    )
    residual_cols = previous_columns.astype(jnp.float32) - product
    scaled = residual_cols / jnp.sqrt(pivot_diag)[None, :]
    new_vectors = scaled.astype(jnp.bfloat16)
    diag_out = diagonal - jnp.sum(scaled * scaled, axis=1)
    return (new_vectors, diag_out, next_columns)


def solution(mesh):
    return jax.shard_map(
        body,
        mesh=mesh,
        in_specs=(
            P(("cols", "sub"), ("groups", "rows")),
            P(("groups", "rows", "cols", "sub"), None),
            P("groups"),
            P(("groups", "rows", "cols", "sub")),
            P(("groups", "rows", "cols", "sub"), None, None),
            P(("groups", "rows", "cols", "sub"), None),
            P("groups", None),
            P("groups"),
            P(),
        ),
        out_specs=(
            P(("groups", "rows", "cols", "sub"), None),
            P(("groups", "rows", "cols", "sub")),
            P(("groups", "rows", "cols", "sub"), None),
        ),
        check_vma=False,
    )
```

profile of v0, /device:TPU:0, one launch (start us, length us, event | category | flops | bytes accessed | tf_op | source)
XLA Modules:
  0.0 100.1 jit_solution(16816415105481037228)
XLA Ops:
  7.2 0.0 reduce-scatter.2.cloned.1.call-start
  7.2 0.0 copy-start.6
  7.2 1.7 %copy.26 = bf16[768,1024]{0,1:T(8,128)(2,1)S(1)} copy(bf16[768,1024]{1,0:T(8,128)(2,1)} %param.9) | data formatting | bytes 3145728 | tf_op args[0]
  9.0 0.0 copy-done.6
  9.0 1.2 %gather_fusion = bf16[256,768]{1,0:T(8,128)(2,1)S(1)} fusion(bf16[768,1024]{0,1:T(8,128)(2,1)S(1)} %copy.26, s32[1024]{0:T(1024)S(1)} %pad_clamp_fusion.1), kind=kCustom, calls=%fused_computation | custom fusion | bytes 787456 | tf_op jit(solution)/shard_map/jit(_take)/gather | solution.py:53
  10.2 0.0 copy-start.1
  10.2 0.2 select_bitcast_fusion
  10.4 37.4 %all-reduce.1 = bf16[768,256]{0,1:T(8,128)(2,1)S(1)} all-reduce(f32[768,256]{0,1:T(8,128)S(1)} %select_bitcast_fusion), channel_id=1, replica_groups=mesh['groups'=2,'rows'=4,'cols'=2,'sub'=2] {'rows'}, use_global_device_ids=true, to_apply=%region_0.1 | all-reduce | flops 196608 | bytes 1179648 | tf_op jit(solution)/shard_map/psum | solution.py:55
  47.8 0.0 copy-done.1
  47.8 0.0 copy-start.7
  47.8 0.0 copy-start.8
  47.9 0.0 copy-start.2
  47.9 1.6 %convolution_bitcast_fusion = f32[1024,256]{0,1:T(8,128)} fusion(bf16[768,1024]{1,0:T(8,128)(2,1)S(1)} %copy-done.1, bf16[768,256]{0,1:T(8,128)(2,1)S(1)} %all-reduce.1), kind=kOutput, calls=%fused_computation.5 | convolution fusion | flops 402653184 | bytes 3014656 | tf_op jit(solution)/shard_map/dot_general | solution.py:102
  49.4 0.0 copy-start.4
  49.4 0.0 copy-start
  49.4 0.0 reduce-scatter.2.cloned.1.call-update
  49.5 0.0 copy-done.7
  49.5 0.0 copy-done.8
  49.5 0.1 select_reduce_fusion.1
  49.6 0.0 copy-done.2
  49.6 0.0 copy-start.5
  49.6 0.0 copy-start.3
  49.6 0.1 fusion.1
  49.7 0.2 copy.30
  50.0 0.2 copy-done.4
  50.1 0.2 dynamic-slice_reduce_fusion
  50.3 0.0 copy-done
  50.3 0.6 dynamic_slice.9
  50.9 0.6 iota_compare_fusion.6
  51.6 0.2 convert_reduce_fusion.1
  51.8 0.3 convolution_convert_fusion
  52.1 0.7 copy.34
  52.8 3.4 %all-to-all-start = ((bf16[4,1,128,256]{3,2,1,0:T(8,128)(2,1)}), bf16[4,1,128,256]{3,2,1,0:T(8,128)(2,1)S(1)}, u32[]{:S(2)}, u32[]{:S(2)}) async-start(bf16[4,1,128,256]{3,2,1,0:T(8,128)(2,1)} %bitcast.26), calls=%async_computation.1 | async-start | bytes 524288 | tf_op jit(solution)/shard_map/all_to_all | solution.py:74
  56.2 0.1 copy.27
  56.3 0.6 gather_fusion.2
  57.0 0.6 gather_fusion.1
  57.6 0.1 compare_and_fusion
  57.6 0.2 convert_reduce_fusion
  57.9 0.0 copy-done.5
  57.9 0.1 select_reduce_fusion
  58.0 31.2 %psum.15 = f32[256]{0:T(256)S(1)} all-reduce(f32[256]{0:T(256)S(1)} %select_reduce_fusion), channel_id=1, replica_groups=mesh['groups'=2,'rows'=4,'cols'=2,'sub'=2] {'rows','cols','sub'}, use_global_device_ids=true, to_apply=%region_3.4 | all-reduce | flops 256 | bytes 2048 | tf_op jit(solution)/shard_map/psum | solution.py:49
  89.2 0.0 copy-done.3
  89.2 0.1 copy.25
  89.3 0.1 add_select_fusion.2
  89.4 0.2 fusion.4
  89.5 0.0 all-to-all-done
  89.6 0.2 copy.32
  89.8 0.3 convolution_convert_fusion.1
  90.1 0.7 reshape.328
  90.8 0.0 reduce-scatter.2.cloned.1.call-done
  90.8 1.1 %multiply_reduce_fusion = (f32[256]{0:T(256)S(1)}, bf16[256,256]{0,1:T(8,128)(2,1)S(1)}) fusion(f32[256]{0:T(256)S(1)} %sqrt.3, f32[256,256]{0,1:T(8,128)} %reduce-scatter.2.cloned.1.call-done, bf16[256,256]{0,1:T(8,128)(2,1)S(1)} %copy.25), kind=kLoop, calls=%fused_computation.11 | loop fusion | flops 392960 | bytes 526336 | tf_op jit(solution)/shard_map/reduce_sum | solution.py:112
  91.9 0.8 copy.29
  92.6 0.6 sub.35
  (11 shorter events, 0.1 us)
Async XLA Ops:
  7.2 83.6 %reduce-scatter.2.cloned.1.call-start = ((), (), s32[]{:S(2)}) async-start(), calls=%async_computation.2 | async-start | bytes 1310720 | tf_op jit(solution)/shard_map/reduce_scatter | solution.py:101
  7.2 1.7 %copy-start.6 = (s32[256]{0:T(256)S(1)}, s32[256]{0:T(256)}, u32[]{:S(2)}) copy-start(s32[256]{0:T(256)} %param.11) | copy-start | bytes 3076
  10.2 37.6 %copy-start.1 = (bf16[768,1024]{1,0:T(8,128)(2,1)S(1)}, bf16[768,1024]{1,0:T(8,128)(2,1)}, u32[]{:S(2)}) copy-start(bf16[768,1024]{1,0:T(8,128)(2,1)} %param.9) | copy-start | bytes 4718596
  47.8 1.6 %copy-start.7 = (s32[4,128]{1,0:T(4,128)S(1)}, s32[4,128]{1,0:T(4,128)}, u32[]{:S(2)}) copy-start(s32[4,128]{1,0:T(4,128)} %param.14) | copy-start | bytes 6148
  47.8 1.6 %copy-start.8 = (f32[4]{0:T(128)S(1)}, f32[4]{0:T(128)}, u32[]{:S(2)}) copy-start(f32[4]{0:T(128)} %param.17) | copy-start | bytes 52
  47.9 1.7 %copy-start.2 = (bf16[4,128,256]{2,1,0:T(8,128)(2,1)S(1)}, bf16[4,128,256]{2,1,0:T(8,128)(2,1)}, u32[]{:S(2)}) copy-start(bf16[4,128,256]{2,1,0:T(8,128)(2,1)} %param.13) | copy-start | bytes 786436
  49.4 0.7 copy-start.4
  49.4 0.9 copy-start
  49.6 8.3 %copy-start.5 = (f32[256]{0:T(256)S(1)}, f32[256]{0:T(256)}, u32[]{:S(2)}) copy-start(f32[256]{0:T(256)} %param.12) | copy-start | bytes 3076
  49.6 39.6 %copy-start.3 = (bf16[256,256]{1,0:T(8,128)(2,1)S(1)}, bf16[256,256]{1,0:T(8,128)(2,1)}, u32[]{:S(2)}) copy-start(bf16[256,256]{1,0:T(8,128)(2,1)} %param.10) | copy-start | bytes 393220
  52.8 36.7 %all-to-all-start = ((bf16[4,1,128,256]{3,2,1,0:T(8,128)(2,1)}), bf16[4,1,128,256]{3,2,1,0:T(8,128)(2,1)S(1)}, u32[]{:S(2)}, u32[]{:S(2)}) async-start(bf16[4,1,128,256]{3,2,1,0:T(8,128)(2,1)} %bitcast.26), calls=%async_computation.1 | async-start | bytes 524288 | tf_op jit(solution)/shard_map/all_to_all | solution.py:74
Sparse Core Ops, SparseCore 0:
  49.6 24.2 reduce-scatter.1
where the time goes:
time: 100 us
  blocking collectives  68.6 us (69%)
  between operations  14.3 us (14%)
  local copies, waits for them, and re-layouts  7.74 us (8%)
  other arithmetic  3.79 us (4%)
  starting transfers between devices  3.44 us (3%)
  matrix products  2.14 us (2%)
    psum x1, blocking collectives, body(): pivot_rows = lax.psum(picked, 'rows').astype(jnp.bfloat16)  37.4 us
    psum x1, blocking collectives, body(): pivot_diag = lax.psum(diag_terms, ('rows', 'cols', 'sub'))  31.2 us
    unnamed x25, local copies, waits for them, and re-layouts  4.02 us
    all_to_all x1, starting transfers between devices, body(): lax.all_to_all(outgoing, 'rows', split_axis=0, concat_axis=0, tiled=True)  3.4 us
  transfers between devices with their start and end apart: 2, of which 0 were waited for; matrix products, arithmetic and copies ran while one was open for 6% of the time, Pallas kernels for 0%

commit v1 on v0

--- a/solution.py
+++ b/solution.py
@@ -1,7 +1,15 @@
+import functools
 import jax
 import jax.numpy as jnp
 from jax import lax
 from jax.sharding import PartitionSpec as P
+
+
+def shapes_place(matrix, link_axis, device_axis):
+    return lax.psum(lax.psum(matrix, link_axis), device_axis)
+
+
+_name_rails = functools.partial(shapes_place, link_axis=("cols", "sub"), device_axis="rows")
 
 
 def slot_plan(row_targets, count, column_size, per_device):
@@ -46,7 +54,7 @@
     local_pivots = pivots - device_index * rows_here
     matches = jnp.arange(rows_here, dtype=jnp.int32)[:, None] == local_pivots[None, :]
     diag_terms = jnp.sum(jnp.where(matches, diagonal[:, None], jnp.float32(0.0)), axis=0)
-    pivot_diag = lax.psum(diag_terms, ("rows", "cols", "sub"))
+    pivot_diag = _name_rails(diag_terms)
     band_pivots = pivots - band_index * band_rows
     inside = (band_pivots >= 0) & (band_pivots < band_rows)
     clamped = jnp.clip(band_pivots, 0, band_rows - 1)

time: 100 us -> 91 us (0.910)
  blocking collectives: 68.6 us -> 44.7 us
  waiting for transfers between devices: 0.02 us -> 13.1 us
  other arithmetic: 3.79 us -> 5.15 us
    psum x2, blocking collectives: 68.6 us -> 44.7 us  [shapes_place(): return lax.psum(lax.psum(matrix, link_axis), device_axis)]
    reduce_scatter x1, waiting for transfers between devices: 0.01 us -> 8.34 us  [body(): lax.psum_scatter(lax.dot_general(stored_vectors, pivot_rows, (((0,), (0,)...]
    all_to_all x1, waiting for transfers between devices: 0.01 us -> 4.73 us  [body(): lax.all_to_all(outgoing, 'rows', split_axis=0, concat_axis=0, tiled=True)]
  transfers between devices with their start and end apart: 2 -> 2, of which waited for: 0 -> 2; matrix products, arithmetic and copies ran while one was open for 6% -> 7% of each run, Pallas kernels for 0% -> 0%
where the time goes in v1:
time: 91 us; the launch traced here: 90.6 us
  blocking collectives  44.7 us (49%)
  between operations  14.3 us (16%)
  waiting for transfers between devices  13.1 us (14%)
  local copies, waits for them, and re-layouts  7.77 us (9%)
  other arithmetic  5.15 us (6%)
  starting transfers between devices  3.45 us (4%)
  matrix products  2.14 us (2%)
    psum x2, blocking collectives, shapes_place(): return lax.psum(lax.psum(matrix, link_axis), device_axis)  44.7 us
    reduce_scatter x1, waiting for transfers between devices, body(): lax.psum_scatter(lax.dot_general(stored_vectors, pivot_rows, (((0,), (0,)...  8.34 us
    all_to_all x1, waiting for transfers between devices, body(): lax.all_to_all(outgoing, 'rows', split_axis=0, concat_axis=0, tiled=True)  4.73 us
    unnamed x25, local copies, waits for them, and re-layouts  4.05 us
    all_to_all x1, starting transfers between devices, body(): lax.all_to_all(outgoing, 'rows', split_axis=0, concat_axis=0, tiled=True)  3.41 us
  transfers between devices with their start and end apart: 2, of which 2 were waited for; matrix products, arithmetic and copies ran while one was open for 7% of the time, Pallas kernels for 0%

profile of v1, /device:TPU:0, one launch (start us, length us, event | category | flops | bytes accessed | tf_op | source)
XLA Modules:
  0.0 90.6 jit_solution(8050391367534933791)
XLA Ops:
  7.2 0.0 reduce-scatter.2.cloned.1.call-start
  7.2 0.7 broadcast_subtract_fusion
  7.9 0.8 select_reduce_fusion
  8.7 8.4 %psum.22 = f32[256]{0:T(256)S(1)} all-reduce(f32[256]{0:T(256)S(1)} %select_reduce_fusion), channel_id=1, replica_groups=mesh['groups'=2,'rows'=4,'cols'=2,'sub'=2] {'cols','sub'}, use_global_device_ids=true, to_apply=%region_3.4 | all-reduce | flops 256 | bytes 2048 | tf_op jit(solution)/shard_map/psum | solution.py:9
  17.1 0.0 copy-start.6
  17.1 1.7 %copy.26 = bf16[768,1024]{0,1:T(8,128)(2,1)S(1)} copy(bf16[768,1024]{1,0:T(8,128)(2,1)} %param.9) | data formatting | bytes 3145728 | tf_op args[0]
  18.8 0.0 copy-done.6
  18.8 1.2 %gather_fusion = bf16[256,768]{1,0:T(8,128)(2,1)S(1)} fusion(bf16[768,1024]{0,1:T(8,128)(2,1)S(1)} %copy.26, s32[1024]{0:T(1024)S(1)} %pad_clamp_fusion.1), kind=kCustom, calls=%fused_computation | custom fusion | bytes 787456 | tf_op jit(solution)/shard_map/jit(_take)/gather | solution.py:61
  20.0 0.0 copy-start.1
  20.0 0.2 select_bitcast_fusion
  20.2 36.4 %all-reduce.2 = (f32[256]{0:T(256)S(1)}, bf16[768,256]{0,1:T(8,128)(2,1)S(1)}) all-reduce(f32[256]{0:T(256)S(1)} %psum.22, f32[768,256]{0,1:T(8,128)S(1)} %select_bitcast_fusion), channel_id=1, replica_groups=mesh['groups'=2,'rows'=4,'cols'=2,'sub'=2] {'rows'}, use_global_device_ids=true, to_apply=%region_4.5 | all-reduce | flops 196864 | bytes 1181696 | tf_op jit(solution)/shard_map/psum | solution.py:9
  56.6 0.0 copy-done.1
  56.6 0.0 copy-start.7
  56.6 0.0 copy-start.8
  56.6 0.0 copy-start.2
  56.6 1.6 %convolution_bitcast_fusion = f32[1024,256]{0,1:T(8,128)} fusion(bf16[768,1024]{1,0:T(8,128)(2,1)S(1)} %copy-done.1, bf16[768,256]{0,1:T(8,128)(2,1)S(1)} %get-tuple-element.18), kind=kOutput, calls=%fused_computation.5 | convolution fusion | flops 402653184 | bytes 3014656 | tf_op jit(solution)/shard_map/dot_general | solution.py:110
  58.2 0.0 copy-start.4
  58.2 0.0 copy-start
  58.2 0.0 reduce-scatter.2.cloned.1.call-update
  58.2 0.0 copy-done.7
  58.2 0.0 copy-done.8
  58.3 0.1 select_reduce_fusion.1
  58.3 0.0 copy-done.2
  58.3 0.0 copy-start.3
  58.4 0.1 fusion.1
  58.5 0.2 copy.30
  58.7 0.2 copy-done.4
  58.9 0.2 dynamic-slice_reduce_fusion
  59.1 0.0 copy-done
  59.1 0.6 dynamic_slice.9
  59.7 0.6 iota_compare_fusion.6
  60.4 0.2 convert_reduce_fusion.1
  60.5 0.3 convolution_convert_fusion
  60.8 0.7 copy.34
  61.6 3.4 %all-to-all-start = ((bf16[4,1,128,256]{3,2,1,0:T(8,128)(2,1)}), bf16[4,1,128,256]{3,2,1,0:T(8,128)(2,1)S(1)}, u32[]{:S(2)}, u32[]{:S(2)}) async-start(bf16[4,1,128,256]{3,2,1,0:T(8,128)(2,1)} %bitcast.26), calls=%async_computation.1 | async-start | bytes 524288 | tf_op jit(solution)/shard_map/all_to_all | solution.py:82
  65.0 0.0 copy-start.5
  65.0 0.1 copy.27
  65.1 0.6 gather_fusion.2
  65.8 0.6 gather_fusion.1
  66.3 0.1 compare_and_fusion
  66.4 0.2 convert_reduce_fusion
  66.7 0.0 copy-done.3
  66.7 0.1 copy.25
  66.8 0.1 add_select_fusion.2
  66.9 0.2 fusion.4
  67.0 4.7 %all-to-all-done = bf16[4,1,128,256]{3,2,1,0:T(8,128)(2,1)S(1)} async-done(((bf16[4,1,128,256]{3,2,1,0:T(8,128)(2,1)}), bf16[4,1,128,256]{3,2,1,0:T(8,128)(2,1)S(1)}, u32[]{:S(2)}, u32[]{:S(2)}) %all-to-all-start) | async-done | bytes 262176 | tf_op jit(solution)/shard_map/all_to_all | solution.py:82
  71.8 0.2 copy.32
  72.0 0.3 convolution_convert_fusion.1
  72.3 0.7 reshape.328
  73.0 8.3 %reduce-scatter.2.cloned.1.call-done = f32[256,256]{0,1:T(8,128)} async-done(((f32[1024,256]{0,1:T(8,128)}), f32[256,256]{0,1:T(8,128)}) %reduce-scatter.2.cloned.1.call-update) | async-done | bytes 262160 | tf_op jit(solution)/shard_map/reduce_scatter | solution.py:109
  81.3 1.1 %multiply_reduce_fusion = (f32[256]{0:T(256)S(1)}, bf16[256,256]{0,1:T(8,128)(2,1)S(1)}) fusion(f32[256]{0:T(256)S(1)} %sqrt.3, f32[256,256]{0,1:T(8,128)} %reduce-scatter.2.cloned.1.call-done, bf16[256,256]{0,1:T(8,128)(2,1)S(1)} %copy.25), kind=kLoop, calls=%fused_computation.11 | loop fusion | flops 392960 | bytes 526336 | tf_op jit(solution)/shard_map/reduce_sum | solution.py:120
  82.4 0.8 copy.29
  83.2 0.0 copy-done.5
  83.2 0.6 sub.35
  (10 shorter events, 0.1 us)
Async XLA Ops:
  7.2 74.2 %reduce-scatter.2.cloned.1.call-start = ((), (), s32[]{:S(2)}) async-start(), calls=%async_computation.2 | async-start | bytes 1310720 | tf_op jit(solution)/shard_map/reduce_scatter | solution.py:109
  17.1 1.7 %copy-start.6 = (s32[256]{0:T(256)S(1)}, s32[256]{0:T(256)}, u32[]{:S(2)}) copy-start(s32[256]{0:T(256)} %param.11) | copy-start | bytes 3076
  20.0 36.6 %copy-start.1 = (bf16[768,1024]{1,0:T(8,128)(2,1)S(1)}, bf16[768,1024]{1,0:T(8,128)(2,1)}, u32[]{:S(2)}) copy-start(bf16[768,1024]{1,0:T(8,128)(2,1)} %param.9) | copy-start | bytes 4718596
  56.6 1.6 %copy-start.7 = (s32[4,128]{1,0:T(4,128)S(1)}, s32[4,128]{1,0:T(4,128)}, u32[]{:S(2)}) copy-start(s32[4,128]{1,0:T(4,128)} %param.14) | copy-start | bytes 6148
  56.6 1.6 %copy-start.8 = (f32[4]{0:T(128)S(1)}, f32[4]{0:T(128)}, u32[]{:S(2)}) copy-start(f32[4]{0:T(128)} %param.17) | copy-start | bytes 52
  56.6 1.7 %copy-start.2 = (bf16[4,128,256]{2,1,0:T(8,128)(2,1)S(1)}, bf16[4,128,256]{2,1,0:T(8,128)(2,1)}, u32[]{:S(2)}) copy-start(bf16[4,128,256]{2,1,0:T(8,128)(2,1)} %param.13) | copy-start | bytes 786436
  58.2 0.7 copy-start.4
  58.2 0.9 copy-start
  58.3 8.3 %copy-start.3 = (bf16[256,256]{1,0:T(8,128)(2,1)S(1)}, bf16[256,256]{1,0:T(8,128)(2,1)}, u32[]{:S(2)}) copy-start(bf16[256,256]{1,0:T(8,128)(2,1)} %param.10) | copy-start | bytes 393220
  61.6 10.2 %all-to-all-start = ((bf16[4,1,128,256]{3,2,1,0:T(8,128)(2,1)}), bf16[4,1,128,256]{3,2,1,0:T(8,128)(2,1)S(1)}, u32[]{:S(2)}, u32[]{:S(2)}) async-start(bf16[4,1,128,256]{3,2,1,0:T(8,128)(2,1)} %bitcast.26), calls=%async_computation.1 | async-start | bytes 524288 | tf_op jit(solution)/shard_map/all_to_all | solution.py:82
  65.0 18.2 %copy-start.5 = (f32[256]{0:T(256)S(1)}, f32[256]{0:T(256)}, u32[]{:S(2)}) copy-start(f32[256]{0:T(256)} %param.12) | copy-start | bytes 3076
Sparse Core Ops, SparseCore 0:
  58.4 22.9 reduce-scatter.1
